TPU v7x, 32 devices: a whole 2x2x4 slice. The times are simulated.
32 devices in a mesh: ep: 8 (over z, y), dp: 4 (over x, core).
Axes of the slice: x: 2, y: 2, z: 4, core: 2. Of those that a mesh axis runs over, the one named last changes fastest.
Arguments:
- tokens: bfloat16 [6144, 2880], P(('ep', 'dp')), may hold values from -64 to 64
- out_grad: bfloat16 [6144, 2880], P(('ep', 'dp')), may hold values from -6 to 6
- indices: int32 [6144, 4], P(('ep', 'dp')), may hold values from 0 to 31, as said below
- expert_rows: bfloat16 [4, 32, 8, 36, 2880], P('dp', 'ep'), may hold values from -0.111328125 to 0.111328125
- router_weight: bfloat16 [2880, 32], replicated, may hold values from -1 to 1
- router_bias: float32 [32], replicated, may hold values from -3 to 3
- balance_scale: float32 [1], replicated, may hold values from 64 to 256
Outputs:
- token_grad: bfloat16 [6144, 2880], P(('ep', 'dp'))
- weight_grad: float32 [2880, 32], P('dp', 'ep')
- balance_loss: float32 [1], replicated
Inputs may be any that keep to these rules, and one draw needn't show every extreme that they name: `indices`: each row names 4 different experts. Within the 192 rows of one device no expert is named by more than 36 rows, and some expert is named by exactly 36 rows. Within the rows of one device the 4 experts of one ep index (experts j * 4 to j * 4 + 3) are named by at most 108 rows together, and those of some ep index by exactly 108. Every expert is named by some row of every device.
All inputs are finite; a program needn't handle non-finite values.
Results may differ from a plain program's by a relative error of at most 0.0014.
The roundings to bfloat16 on the way count: a program that leaves them out, or rounds other values in their place, can miss the bound.
Values may be sent and summed in bfloat16 or wider, within the bound.
A program may use at most 128 MiB of HBM per device.

v0:
```python
import math

import jax
import jax.numpy as jnp
from jax import lax
from jax.sharding import PartitionSpec as P


def on_device(tokens, out_grad, indices, expert_rows, router_weight, router_bias, balance_scale):
    tok_dev = tokens.shape[0]
    chosen = indices.shape[1]
    width = tokens.shape[1]
    experts = router_weight.shape[1]
    capacity = expert_rows.shape[3]
    ep_size = lax.axis_size("ep")
    dp_size = lax.axis_size("dp")
    token_total = tok_dev * ep_size * dp_size
    expert_ids = jnp.arange(experts, dtype=jnp.int32)
    onehot = (indices[:, :, None] == expert_ids[None, None, :]).astype(jnp.float32)
    named_by = jnp.sum(onehot, axis=1)
    local_counts = jnp.sum(named_by, axis=0)
    logits = jnp.dot(tokens, router_weight, preferred_element_type=jnp.float32) + router_bias
    probability = jax.nn.softmax(logits, axis=-1)
    counts, prob_sums = lax.psum((local_counts, jnp.sum(probability, axis=0)), ("ep", "dp"))
    share_of = counts / (token_total * chosen)
    balance_loss = (experts * jnp.sum(share_of * (prob_sums / token_total))).reshape(1)
    row_ids = jnp.arange(tok_dev, dtype=jnp.int32)
    lower_mask = (row_ids[:, None] > row_ids[None, :]).astype(jnp.bfloat16)
    before = jnp.dot(lower_mask, named_by.astype(jnp.bfloat16), preferred_element_type=jnp.float32)
    slot_index = jnp.sum(onehot * before[:, None, :], axis=2).astype(jnp.int32)
    returned = lax.all_to_all(expert_rows, "ep", split_axis=2, concat_axis=1, tiled=True)
    flat_rows = returned.reshape(experts * capacity, width)
    row_index = indices * capacity + slot_index
    picked = jnp.take(flat_rows, row_index, axis=0)
    pair_dots = jnp.einsum("td,tkd->tk", out_grad, picked, preferred_element_type=jnp.float32)
    chosen_logits = jnp.take_along_axis(logits, indices, axis=1)
    mix_weight = jax.nn.softmax(chosen_logits, axis=-1)
    sel_grad = mix_weight * (pair_dots - jnp.sum(mix_weight * pair_dots, axis=1, keepdims=True))
    balance_push = balance_scale[0] * experts * share_of
    spread = probability * (
        balance_push[None, :] - jnp.sum(probability * balance_push[None, :], axis=1, keepdims=True)
    )
    logit_grad = (spread + jnp.sum(onehot * sel_grad[:, :, None], axis=1)).astype(jnp.bfloat16)
    token_grad = lax.dot_general(
        logit_grad, router_weight, (((1,), (1,)), ((), ())), preferred_element_type=jnp.float32
    ).astype(jnp.bfloat16)
    term = lax.dot_general(
        tokens, logit_grad, (((0,), (0,)), ((), ())), preferred_element_type=jnp.float32
    )
    summed = lax.psum_scatter(term, "ep", scatter_dimension=1, tiled=True)
    summed = lax.psum_scatter(summed, "dp", scatter_dimension=0, tiled=True)
    weight_grad = summed / math.sqrt(token_total)
    return (token_grad, weight_grad, balance_loss)


def solution(mesh):
    placed = (
        P(("ep", "dp"), None),
        P(("ep", "dp"), None),
        P(("ep", "dp"), None),
        P("dp", "ep", None, None, None),
        P(),
        P(),
        P(),
    )
    return jax.shard_map(
        on_device,
        mesh=mesh,
        in_specs=placed,
        out_specs=(P(("ep", "dp"), None), P("dp", "ep"), P()),
        check_vma=False,
    )
```

profile of v0, /device:TPU:0, one launch (start us, length us, event | category | flops | bytes accessed | tf_op | source)
XLA Modules:
  0.0 366.3 jit_solution(14106931418418347998)
XLA Ops:
  7.2 0.0 copy-start
  7.2 7.0 %copy.48 = bf16[1,4,8,36,2880]{4,3,1,0,2:T(8,128)(2,1)} copy(bf16[1,4,8,36,2880]{4,2,3,1,0:T(8,128)(2,1)} %param.10) | data formatting | bytes 13271040 | tf_op args[3]
  14.2 0.0 copy-start.3
  14.2 0.0 copy-start.2
  14.2 0.0 copy-start.4
  14.2 7.5 %all-to-all-start = ((bf16[1,4,8,36,2880]{4,3,1,0,2:T(8,128)(2,1)}), bf16[1,4,8,36,2880]{4,3,1,0,2:T(8,128)(2,1)}, u32[]{:S(2)}, u32[]{:S(2)}) async-start(bf16[1,4,8,36,2880]{4,3,1,0,2:T(8,128)(2,1)} %copy.48), calls=%async_computation | async-start | bytes 15073280 | tf_op jit(solution)/shard_map/all_to_all | solution.py:31
  21.7 0.0 all-reduce.3.cloned.1.call-start
  21.7 0.0 copy-done.3
  21.8 0.1 fusion.5
  21.9 0.2 convert_reduce_fusion.1
  22.1 184.7 %psum.14 = f32[32]{0:T(128)S(1)} all-reduce(f32[32]{0:T(128)S(1)} %get-tuple-element.5), channel_id=1, replica_groups=mesh['ep'=8,'dp'=4] {'ep','dp'}, use_global_device_ids=true, to_apply=%region_3.0 | all-reduce | flops 32 | bytes 256 | tf_op jit(solution)/shard_map/psum | solution.py:24
  206.8 0.1 copy.49
  206.9 0.1 reshape.45
  207.0 0.2 copy.47
  207.2 0.1 copy.45
  207.3 0.1 reshape.51
  207.4 0.0 copy-done.1
  207.4 0.0 copy-done.2
  207.4 0.0 copy-done.4
  207.4 0.5 fusion.16
  207.9 6.3 %gather_fusion.1 = f32[768]{0:T(1024)S(1)} fusion(f32[192,32]{0,1:T(8,128)S(1)} %get-tuple-element.12, s32[768]{0:T(1024)S(1)} %reshape.51), kind=kCustom, calls=%fused_computation.1 | custom fusion | bytes 12288 | tf_op jit(solution)/shard_map/jit(take_along_axis)/gather | solution.py:36
  214.3 0.1 reshape.54
  214.4 0.1 copy.46
  215.2 0.1 fusion.14
  215.4 0.0 all-to-all-done
  215.4 9.3 %reshape.41 = bf16[1152,2880]{1,0:T(8,128)(2,1)} reshape(bf16[1,8,4,1,36,2880]{5,4,2,1,3,0:T(8,128)(2,1)} %bitcast.3) | data formatting | bytes 13271040 | tf_op jit(solution)/shard_map/reshape | solution.py:32
  224.7 13.1 %gather_fusion = bf16[768,2880]{1,0:T(8,128)(2,1)} fusion(bf16[1152,2880]{1,0:T(8,128)(2,1)} %reshape.41, s32[1024]{0:T(1024)S(1)} %pad_clamp_fusion), kind=kCustom, calls=%fused_computation | custom fusion | bytes 8850432 | tf_op jit(solution)/shard_map/jit(_take)/gather | solution.py:34
  237.8 7.1 %reshape.44 = bf16[192,4,2880]{2,1,0:T(4,128)(2,1)} reshape(bf16[768,2880]{1,0:T(8,128)(2,1)} %gather_fusion) | data formatting | bytes 8847360 | tf_op jit(solution)/shard_map/jit(_take)/gather | solution.py:34
  244.9 0.0 copy-done
  244.9 0.0 copy-start.5
  244.9 9.4 %fusion = f32[192,1,4]{2,1,0:T(1,128)S(1)} fusion(bf16[192,4,2880]{2,1,0:T(4,128)(2,1)} %reshape.44, pred[192,4]{1,0:T(8,128)(4,1)S(1)} %copy.47, bf16[192,2880,1]{1,0,2:T(8,128)(2,1)S(1)} %bitcast.30), kind=kOutput, calls=%fused_computation.2 | convolution fusion | flops 6635520 | bytes 5533440 | tf_op jit(solution)/shard_map/td,tkd->tk/dot_general | solution.py:35
  254.3 0.1 copy.51
  254.5 0.1 add_convert_fusion
  254.6 1.1 convolution_bitcast_fusion
  255.7 0.0 all-reduce.3.cloned.1.call-update
  255.7 0.0 reduce-scatter.4.cloned.1.call-start
  255.7 39.3 %psum.15 = f32[32]{0:T(128)S(1)} all-reduce(f32[32]{0:T(128)S(1)} %get-tuple-element.3), channel_id=1, replica_groups=mesh['ep'=8,'dp'=4] {'ep','dp'}, use_global_device_ids=true, to_apply=%region_14.15 | all-reduce | flops 32 | bytes 256 | tf_op jit(solution)/shard_map/psum | solution.py:24
  295.0 0.0 copy-done.5
  295.0 0.6 dynamic-slice
  296.3 0.6 multiply_reduce_fusion.1
  297.5 29.8 %all-reduce.3.cloned.1.call-done = f32[2880,32]{0,1:T(8,128)} async-done(((f32[2880,32]{0,1:T(8,128)}), f32[2880,32]{0,1:T(8,128)}) %all-reduce.3.cloned.1.call-update) | async-done | bytes 368656
  327.3 0.9 constant_dynamic-slice_fusion
  328.2 1.6 copy.52
  329.9 0.0 reduce-scatter.4.cloned.1.call-update
  329.9 1.5 convolution_convert_fusion
  331.4 25.2 %reduce-scatter.4.cloned.1.call-done = f32[720,4]{1,0:T(8,128)} async-done(((f32[2880,4]{1,0:T(8,128)}), f32[720,4]{1,0:T(8,128)}) %reduce-scatter.4.cloned.1.call-update) | async-done | bytes 11536
  356.6 1.1 copy.53
  357.7 0.6 broadcast_multiply_fusion
  (12 shorter events, 0.2 us)
Async XLA Ops:
  7.2 237.8 %copy-start = (bf16[192,2880]{1,0:T(8,128)(2,1)S(1)}, bf16[192,2880]{1,0:T(8,128)(2,1)}, u32[]{:S(2)}) copy-start(bf16[192,2880]{1,0:T(8,128)(2,1)} %param.8) | copy-start | bytes 3317764
  14.2 7.5 %copy-start.3 = (s32[192,4]{0,1:T(4,128)S(1)}, s32[192,4]{0,1:T(4,128)}, u32[]{:S(2)}) copy-start(s32[192,4]{0,1:T(4,128)} %param.9) | copy-start | bytes 9220
  14.2 193.2 %copy-start.1 = (bf16[192,2880]{1,0:T(8,128)(2,1)S(1)}, bf16[192,2880]{1,0:T(8,128)(2,1)}, u32[]{:S(2)}) copy-start(bf16[192,2880]{1,0:T(8,128)(2,1)} %param.7) | copy-start | bytes 3317764
  14.2 193.2 %copy-start.2 = (bf16[2880,32]{0,1:T(8,128)(2,1)S(1)}, bf16[2880,32]{0,1:T(8,128)(2,1)}, u32[]{:S(2)}) copy-start(bf16[2880,32]{0,1:T(8,128)(2,1)} %param.11) | copy-start | bytes 552964
  14.2 193.2 %copy-start.4 = (f32[32]{0:T(128)S(1)}, f32[32]{0:T(128)}, u32[]{:S(2)}) copy-start(f32[32]{0:T(128)} %param.12) | copy-start | bytes 388
  14.2 201.1 %all-to-all-start = ((bf16[1,4,8,36,2880]{4,3,1,0,2:T(8,128)(2,1)}), bf16[1,4,8,36,2880]{4,3,1,0,2:T(8,128)(2,1)}, u32[]{:S(2)}, u32[]{:S(2)}) async-start(bf16[1,4,8,36,2880]{4,3,1,0,2:T(8,128)(2,1)} %copy.48), calls=%async_computation | async-start | bytes 15073280 | tf_op jit(solution)/shard_map/all_to_all | solution.py:31
  21.7 305.6 %all-reduce.3.cloned.1.call-start = ((), (), s32[]{:S(2)}) async-start(), calls=%async_computation.3 | async-start | bytes 753664
  244.9 50.1 %copy-start.5 = (u32[32]{0:T(128)S(1)}, u32[32]{0:T(128)}, u32[]{:S(2)}) copy-start(u32[32]{0:T(128)} %constant.70) | copy-start | bytes 388
  255.7 100.9 %reduce-scatter.4.cloned.1.call-start = ((), (), s32[]{:S(2)}) async-start(), calls=%async_computation.2 | async-start | bytes 1843200
Sparse Core Ops, SparseCore 0:
  255.8 71.4 all-reduce.2
  330.0 26.5 reduce-scatter.3
where the time goes:
time: 367 us; the launch traced here: 366 us
  blocking collectives  224 us (61%)
  waiting for transfers between devices  55.1 us (15%)
  local copies, waits for them, and re-layouts  48.1 us (13%)
  between operations  17.3 us (5%)
  matrix products  12.6 us (3%)
  starting transfers between devices  7.53 us (2%)
    psum x2, blocking collectives, on_device(): lax.psum((local_counts, jnp.sum(probability, axis=0)), ('ep', 'dp'))  224 us
    unnamed x4, waiting for transfers between devices  55.1 us
    gather x2, local copies, waits for them, and re-layouts, on_device(): picked = jnp.take(flat_rows, row_index, axis=0)  20.2 us
    unnamed x17, local copies, waits for them, and re-layouts  11.3 us
    dot_general x1, matrix products, on_device(): jnp.einsum('td,tkd->tk', out_grad, picked, preferred_element_type=jnp.flo...  9.4 us
    reshape x1, local copies, waits for them, and re-layouts, on_device(): flat_rows = returned.reshape(experts * capacity, width)  9.32 us
    all_to_all x1, starting transfers between devices, on_device(): lax.all_to_all(expert_rows, 'ep', split_axis=2, concat_axis=1, tiled=True)  7.45 us
  transfers between devices with their start and end apart: 3, of which 2 were waited for; matrix products, arithmetic and copies ran while one was open for 3% of the time, Pallas kernels for 0%

commit v1 on v0

v1 whole, which is shorter than its diff:
```python
import functools
import math

import jax
import jax.numpy as jnp
from jax import lax
from jax.experimental import pallas as pl
from jax.experimental.pallas import tpu as pltpu
from jax.sharding import PartitionSpec as P

MESH = pl.DeviceIdType.MESH
F32 = jnp.float32
BF16 = jnp.bfloat16
CHUNK = 768


def dot_nt(x, y, precision=None):
    return lax.dot_general(
        x, y, (((1,), (1,)), ((), ())), preferred_element_type=F32, precision=precision
    )


def dot_nn(x, y, precision=None):
    return lax.dot_general(
        x, y, (((1,), (0,)), ((), ())), preferred_element_type=F32, precision=precision
    )


def kernel(cfg, *refs):
    ep, dp, tok_dev, chosen, experts, exp_dev, cap, packed, widths, token_total = cfg
    line = ep // 2
    chunks = len(widths)
    starts = [sum(widths[:c]) for c in range(chunks)]
    (idx_in, grad_in, rows_in, tok_in, wt_in, bias_in, scale_in, lg_out, wg_out, loss_out) = refs[:10]
    refs = refs[10:]
    xb = refs[:chunks]
    lsend = refs[chunks:2 * chunks]
    lrecv = refs[2 * chunks:3 * chunks]
    (rows_v, idx_all, pin, pout, tgt_x, tgt_p, acc_x, acc_p, rst, rbuf, tks, tkr, logit_v, prob_v,
     named_v, st_dp, st_ep, lgd, ws, wr,
     s_rows, s_own, s_idx, r_idx, s_right, s_left, r_x, s_leaf, r_leaf, s_rep, r_rep,
     s_tk, r_tk, s_sd, r_sd, s_se, r_se, s_lg, r_lg, s_w, r_w) = refs[3 * chunks:]
    me = lax.axis_index("ep")
    md = lax.axis_index("dp")
    pos = me // 2
    side = lax.rem(me, 2)
    mate = pos * 2 + 1 - side

    def ep_id(other):
        return (other, md)

    def remote(src, dst, s, r, dev):
        return pltpu.make_async_remote_copy(
            src_ref=src, dst_ref=dst, send_sem=s, recv_sem=r, device_id=dev, device_id_type=MESH
        )

    def ep_peer(s):
        return lax.rem(me + s, ep)

    def dp_peer(s):
        return lax.rem(md + s, dp)

    own = [
        pltpu.make_async_copy(grad_in.at[:, pl.ds(starts[c], widths[c])], xb[c].at[pos], s_own.at[c])
        for c in range(chunks)
    ]
    for copy in own:
        copy.start()
    rows_copy = pltpu.make_async_copy(rows_in.at[0], rows_v, s_rows)
    rows_copy.start()

    barrier = pltpu.get_barrier_semaphore()

    def greet(s, carry):
        pl.semaphore_signal(barrier, inc=1, device_id=ep_id(ep_peer(s)), device_id_type=MESH)
        return carry

    lax.fori_loop(1, ep, greet, 0)
    for s in range(1, dp):
        pl.semaphore_signal(barrier, inc=1, device_id=(me, dp_peer(s)), device_id_type=MESH)
    pl.semaphore_wait(barrier, ep - 1 + dp - 1)

    def idx_copy(s):
        return remote(idx_in, idx_all.at[me], s_idx.at[s], r_idx.at[me], ep_id(ep_peer(s)))

    def idx_arrival(s):
        src = lax.rem(me + ep - s, ep)
        return remote(idx_in, idx_all.at[src], s_idx.at[s], r_idx.at[src], ep_id(src))

    def loop_ep(fn):
        def body(s, carry):
            fn(s)
            return carry
        lax.fori_loop(1, ep, body, 0)

    def to_right(q, c):
        return remote(xb[c].at[q], xb[c].at[q], s_right.at[q, c], r_x.at[q, c], ep_id(me + 2))

    def to_left(q, c):
        return remote(xb[c].at[q], xb[c].at[q], s_left.at[q, c], r_x.at[q, c], ep_id(me - 2))

    def leaf(q, c):
        return remote(lsend[c].at[q], lrecv[c].at[q], s_leaf.at[q, c], r_leaf.at[q, c], ep_id(mate))

    def reply(j):
        return remote(rst.at[j], rbuf.at[me], s_rep.at[j], r_rep.at[me], ep_id(j))

    loop_ep(lambda s: idx_copy(s).start())
    for c in range(chunks):
        own[c].wait()

        @pl.when(pos < line - 1)
        def _():
            to_right(pos, c).start()

        @pl.when(pos > 0)
        def _():
            to_left(pos, c).start()

    part = tok_in.shape[1] // dp
    for d in range(dp):
        tks[d] = tok_in[:, d * part:(d + 1) * part]

    idx = idx_in[...]
    expert_row = lax.broadcasted_iota(jnp.int32, (experts, tok_dev), 0)
    named = jnp.zeros((experts, tok_dev), F32)
    for k in range(chosen):
        named = named + jnp.where(idx[k:k + 1, :] == expert_row, 1.0, 0.0)
    logits = dot_nt(wt_in[...], tok_in[...]) + bias_in[...]
    top = jnp.max(logits, axis=0, keepdims=True)
    power = jnp.exp(logits - top)
    prob = power / jnp.sum(power, axis=0, keepdims=True)
    logit_v[...] = logits
    prob_v[...] = prob
    named_v[...] = named
    ones = jnp.ones((8, tok_dev), F32)
    count_row = dot_nt(ones, named, lax.Precision.HIGHEST)
    prob_row = dot_nt(ones, prob, lax.Precision.HIGHEST)
    stat_row = lax.broadcasted_iota(jnp.int32, (8, experts), 0)
    st_dp[md] = jnp.where(stat_row == 0, count_row, prob_row)

    def tk_copy(s):
        return remote(tks.at[dp_peer(s)], tkr.at[md], s_tk.at[s], r_tk.at[md], (me, dp_peer(s)))

    def tk_arrival(s):
        src = lax.rem(md + dp - s, dp)
        return remote(tks.at[src], tkr.at[src], s_tk.at[s], r_tk.at[src], (me, src))

    def sd_copy(s):
        return remote(st_dp.at[md], st_dp.at[md], s_sd.at[s], r_sd.at[md], (me, dp_peer(s)))

    def sd_arrival(s):
        src = lax.rem(md + dp - s, dp)
        return remote(st_dp.at[src], st_dp.at[src], s_sd.at[s], r_sd.at[src], (me, src))

    for s in range(1, dp):
        sd_copy(s).start()
    for s in range(1, dp):
        tk_copy(s).start()
    tkr[md] = tks[md]

    t_from = lax.broadcasted_iota(jnp.int32, (tok_dev, tok_dev), 0)
    t_to = lax.broadcasted_iota(jnp.int32, (tok_dev, tok_dev), 1)
    upper = jnp.where(t_from < t_to, 1.0, 0.0).astype(BF16)
    row8 = lax.broadcasted_iota(jnp.int32, (8, tok_dev), 0)
    slot_p = lax.broadcasted_iota(jnp.int32, (packed, tok_dev), 0).astype(F32)

    def plan(table, group):
        who = jnp.where(row8 < exp_dev, group * exp_dev + row8, -2)
        hit = jnp.zeros((8, tok_dev), F32)
        for k in range(chosen):
            hit = hit + jnp.where(table[k:k + 1, :] == who, 1.0, 0.0)
        need = jnp.max(hit, axis=0, keepdims=True)
        stack = jnp.where(row8 == exp_dev, need, hit)
        before = dot_nn(stack.astype(BF16), upper)
        place = jnp.where(need > 0.5, before[exp_dev:exp_dev + 1, :], -1.0)
        target = jnp.where(hit > 0.5, before, -1.0)
        pack = jnp.where(slot_p == place, 1.0, 0.0).astype(BF16)
        return target, pack

    idx_all[me] = idx
    loop_ep(lambda s: idx_arrival(s).wait_recv())

    def plans(q, carry):
        table = idx_all[q * 2 + side]
        target, _ = plan(table, me)
        tgt_x[q] = target
        _, pack = plan(table, mate)
        pout[q] = pack
        target, pack = plan(idx_all[q * 2 + 1 - side], me)
        pin[q] = pack
        tgt_p[q] = dot_nt((target + 1.0).astype(BF16), pack) - 1.0
        acc_x[q] = jnp.zeros((8, tok_dev), F32)
        acc_p[q] = jnp.zeros((8, packed), F32)
        return carry

    lax.fori_loop(0, line, plans, 0)
    rows_copy.wait()

    def gathered(j, c, block, target, count):
        slot = lax.broadcasted_iota(jnp.int32, (cap, count), 0).astype(F32)
        row = lax.broadcasted_iota(jnp.int32, (8, count), 0)
        out = jnp.zeros((8, count), F32)
        for e in range(exp_dev):
            table = rows_v[e, j, :, starts[c]:starts[c] + widths[c]]
            dots = dot_nt(table, block)
            one = jnp.sum(jnp.where(slot == target[e:e + 1, :], dots, 0.0), axis=0, keepdims=True)
            out = jnp.where(row == e, one, out)
        return out

    def give_leaf(q, c):
        lsend[c][q] = dot_nn(pout[q], xb[c][q]).astype(BF16)
        leaf(q, c).start()

    def use_block(q, c):
        acc_x[q] += gathered(q * 2 + side, c, xb[c][q], tgt_x[q], tok_dev)

    def use_leaf(q, c):
        leaf(q, c).wait_recv()
        acc_p[q] += gathered(q * 2 + 1 - side, c, lrecv[c][q], tgt_p[q], packed)

    def answer(j, value):
        rst[j] = value
        reply(j).start()

    def done_block(q):
        answer(q * 2 + side, acc_x[q])

    def done_leaf(q):
        answer(q * 2 + 1 - side, dot_nn(acc_p[q], pin[q].astype(F32), lax.Precision.HIGHEST))

    def leaf_step(s, c):
        def go(q):
            use_leaf(q, c)
            if c == chunks - 1:
                done_leaf(q)
        if s == 0:
            go(pos)
            return

        @pl.when(pos - s >= 0)
        def _():
            go(pos - s)

        @pl.when(pos + s < line)
        def _():
            go(pos + s)

    lag = 2
    steps = [(s, c) for s in range(line) for c in range(chunks)]
    for n, (s, c) in enumerate(steps):
        if s == 0:
            give_leaf(pos, c)
            use_block(pos, c)
            if c == chunks - 1:
                rbuf[me] = acc_x[pos]
        else:
            @pl.when(pos - s >= 0)
            def _():
                q = pos - s
                to_right(q, c).wait_recv()

                @pl.when(pos < line - 1)
                def _():
                    to_right(q, c).start()

            @pl.when(pos + s < line)
            def _():
                q = pos + s
                to_left(q, c).wait_recv()

                @pl.when(pos > 0)
                def _():
                    to_left(q, c).start()

            for q, ok in ((pos - s, pos - s >= 0), (pos + s, pos + s < line)):
                @pl.when(ok)
                def _(q=q):
                    give_leaf(q, c)

            for q, ok in ((pos - s, pos - s >= 0), (pos + s, pos + s < line)):
                @pl.when(ok)
                def _(q=q):
                    use_block(q, c)
                    if c == chunks - 1:
                        done_block(q)
        if n >= lag:
            leaf_step(*steps[n - lag])
        if n == 1:
            for s_ in range(1, dp):
                sd_arrival(s_).wait_recv()
            total = st_dp[0]
            for d in range(1, dp):
                total = total + st_dp[d]
            st_ep[me] = total
            loop_ep(lambda s_: remote(st_ep.at[me], st_ep.at[me], s_se.at[s_], r_se.at[me], ep_id(ep_peer(s_))).start())
    for n in range(len(steps) - lag, len(steps)):
        leaf_step(*steps[n])

    def se_arrival(s_):
        src = lax.rem(me + ep - s_, ep)
        remote(st_ep.at[src], st_ep.at[src], s_se.at[s_], r_se.at[src], ep_id(src)).wait_recv()

    loop_ep(se_arrival)
    stats = lax.fori_loop(1, ep, lambda j, acc: acc + st_ep[j], st_ep[0])
    share = stats[0:1, :] / (token_total * chosen)
    mean = stats[1:2, :] / token_total
    loss_out[...] = experts * jnp.sum(share * mean, axis=1, keepdims=True)
    push_row = scale_in[0] * experts * share
    eye_r = lax.broadcasted_iota(jnp.int32, (experts, experts), 0)
    eye_c = lax.broadcasted_iota(jnp.int32, (experts, experts), 1)
    push = jnp.sum(jnp.where(eye_r == eye_c, push_row, 0.0), axis=1, keepdims=True)
    prob = prob_v[...]
    spread = prob * (push - jnp.sum(prob * push, axis=0, keepdims=True))
    named = named_v[...]
    logits = logit_v[...]
    high = jnp.max(jnp.where(named > 0.5, logits, -jnp.inf), axis=0, keepdims=True)
    mix = jnp.where(named > 0.5, jnp.exp(jnp.minimum(logits - high, 0.0)), 0.0)
    mix = mix / jnp.sum(mix, axis=0, keepdims=True)

    def rep_arrival(s_):
        src = lax.rem(me + ep - s_, ep)
        remote(rst.at[src], rbuf.at[src], s_rep.at[src], r_rep.at[src], ep_id(src)).wait_recv()

    loop_ep(rep_arrival)
    dots = jnp.concatenate([rbuf[j, 0:exp_dev, :] for j in range(ep)], axis=0)
    sel = mix * (dots - jnp.sum(mix * dots, axis=0, keepdims=True))
    grad = (spread + sel).astype(BF16)
    lg_out[...] = grad
    lgd[md] = grad

    def lg_copy(s):
        return remote(lgd.at[md], lgd.at[md], s_lg.at[s], r_lg.at[md], (me, dp_peer(s)))

    def lg_arrival(s):
        src = lax.rem(md + dp - s, dp)
        return remote(lgd.at[src], lgd.at[src], s_lg.at[s], r_lg.at[src], (me, src))

    for s in range(1, dp):
        lg_copy(s).start()
    for s in range(1, dp):
        tk_arrival(s).wait_recv()
    for s in range(1, dp):
        lg_arrival(s).wait_recv()
    term = dot_nn(lgd[0], tkr[0])
    for d in range(1, dp):
        term = term + dot_nn(lgd[d], tkr[d])
    for j in range(ep):
        ws[j] = term[j * exp_dev:(j + 1) * exp_dev, :]
    wr[me] = ws[me]
    loop_ep(lambda s_: remote(ws.at[ep_peer(s_)], wr.at[me], s_w.at[s_], r_w.at[me], ep_id(ep_peer(s_))).start())

    def w_arrival(s_):
        src = lax.rem(me + ep - s_, ep)
        remote(ws.at[src], wr.at[src], s_w.at[s_], r_w.at[src], ep_id(src)).wait_recv()

    loop_ep(w_arrival)
    out = lax.fori_loop(1, ep, lambda j, acc: acc + wr[j], wr[0])
    wg_out[...] = out / math.sqrt(token_total)

    loop_ep(lambda s_: idx_copy(s_).wait_send())
    loop_ep(lambda s_: remote(st_ep.at[me], st_ep.at[me], s_se.at[s_], r_se.at[me], ep_id(ep_peer(s_))).wait_send())
    loop_ep(lambda s_: reply(ep_peer(s_)).wait_send())
    loop_ep(lambda s_: remote(ws.at[ep_peer(s_)], wr.at[me], s_w.at[s_], r_w.at[me], ep_id(ep_peer(s_))).wait_send())
    for s in range(1, dp):
        sd_copy(s).wait_send()
        tk_copy(s).wait_send()
        lg_copy(s).wait_send()

    def drain(q, carry):
        for c in range(chunks):
            leaf(q, c).wait_send()

            @pl.when(jnp.logical_and(q <= pos, pos < line - 1))
            def _():
                to_right(q, c).wait_send()

            @pl.when(jnp.logical_and(q >= pos, pos > 0))
            def _():
                to_left(q, c).wait_send()
        return carry

    lax.fori_loop(0, line, drain, 0)


def on_device(tokens, out_grad, indices, expert_rows, router_weight, router_bias, balance_scale):
    tok_dev, width = tokens.shape
    chosen = indices.shape[1]
    experts = router_weight.shape[1]
    exp_dev, cap = expert_rows.shape[1], expert_rows.shape[3]
    ep = lax.axis_size("ep")
    dp = lax.axis_size("dp")
    line = ep // 2
    packed = -(-min(tok_dev, (exp_dev - 1) * cap) // 16) * 16
    widths = tuple(min(CHUNK, width - s) for s in range(0, width, CHUNK))
    chunks = len(widths)
    cfg = (ep, dp, tok_dev, chosen, experts, exp_dev, cap, packed, widths, tok_dev * ep * dp)
    part = width // dp
    idx_t = jnp.pad(indices.T, ((0, 8 - chosen), (0, 0)), constant_values=-1)
    vmem = pl.BlockSpec(memory_space=pltpu.VMEM)
    hbm = pl.BlockSpec(memory_space=pl.ANY)
    smem = pl.BlockSpec(memory_space=pltpu.SMEM)
    dma = pltpu.SemaphoreType.DMA
    scratch = [pltpu.VMEM((line, tok_dev, w), BF16) for w in widths]
    scratch += [pltpu.VMEM((line, packed, w), BF16) for w in widths]
    scratch += [pltpu.VMEM((line, packed, w), BF16) for w in widths]
    scratch += [
        pltpu.VMEM(expert_rows.shape[1:], BF16),
        pltpu.VMEM((ep, 8, tok_dev), jnp.int32),
        pltpu.VMEM((line, packed, tok_dev), BF16),
        pltpu.VMEM((line, packed, tok_dev), BF16),
        pltpu.VMEM((line, 8, tok_dev), F32),
        pltpu.VMEM((line, 8, packed), F32),
        pltpu.VMEM((line, 8, tok_dev), F32),
        pltpu.VMEM((line, 8, packed), F32),
        pltpu.VMEM((ep, 8, tok_dev), F32),
        pltpu.VMEM((ep, 8, tok_dev), F32),
        pltpu.VMEM((dp, tok_dev, part), BF16),
        pltpu.VMEM((dp, tok_dev, part), BF16),
        pltpu.VMEM((experts, tok_dev), F32),
        pltpu.VMEM((experts, tok_dev), F32),
        pltpu.VMEM((experts, tok_dev), F32),
        pltpu.VMEM((dp, 8, experts), F32),
        pltpu.VMEM((ep, 8, experts), F32),
        pltpu.VMEM((dp, experts, tok_dev), BF16),
        pltpu.VMEM((ep, exp_dev, part), F32),
        pltpu.VMEM((ep, exp_dev, part), F32),
        dma, dma((chunks,)), dma((ep,)), dma((ep,)),
        dma((line, chunks)), dma((line, chunks)), dma((line, chunks)),
        dma((line, chunks)), dma((line, chunks)), dma((ep,)), dma((ep,)),
        dma((dp,)), dma((dp,)), dma((dp,)), dma((dp,)), dma((ep,)), dma((ep,)),
        dma((dp,)), dma((dp,)), dma((ep,)), dma((ep,)),
    ]
    lg, wg, loss = pl.pallas_call(
        functools.partial(kernel, cfg),
        name="router_backward",
        out_shape=(
            jax.ShapeDtypeStruct((experts, tok_dev), BF16),
            jax.ShapeDtypeStruct((exp_dev, part), F32),
            jax.ShapeDtypeStruct((1, 1), F32),
        ),
        in_specs=[vmem, hbm, hbm, vmem, vmem, vmem, smem],
        out_specs=(vmem, vmem, vmem),
        scratch_shapes=scratch,
        compiler_params=pltpu.CompilerParams(
            collective_id=0, has_side_effects=True, vmem_limit_bytes=56 * 1024 * 1024
        ),
    )(idx_t, out_grad, expert_rows, tokens, router_weight.T, router_bias.reshape(experts, 1), balance_scale)
    token_grad = lax.dot_general(
        lg, router_weight, (((0,), (1,)), ((), ())), preferred_element_type=F32
    ).astype(BF16)
    return (token_grad, wg.T, loss.reshape(1))


def solution(mesh):
    placed = (
        P(("ep", "dp"), None),
        P(("ep", "dp"), None),
        P(("ep", "dp"), None),
        P("dp", "ep", None, None, None),
        P(),
        P(),
        P(),
    )
    return jax.shard_map(
        on_device,
        mesh=mesh,
        in_specs=placed,
        out_specs=(P(("ep", "dp"), None), P("dp", "ep"), P()),
        check_vma=False,
    )
```

time: 367 us -> 119 us (0.32)
  blocking collectives: 224 us -> 0 us
  Pallas kernels: 0 us -> 103 us
  waiting for transfers between devices: 55.1 us -> 0 us
  local copies, waits for them, and re-layouts: 48.1 us -> 10.1 us
  between operations: 17.3 us -> 3.05 us
  matrix products: 12.6 us -> 2.2 us
  starting transfers between devices: 7.53 us -> 0 us
    psum x2 -> x0, blocking collectives: 224 us -> none  [on_device(): lax.psum((local_counts, jnp.sum(probability, axis=0)), ('ep', 'dp'))]
    pallas_call x0 -> x1, Pallas kernels: none -> 103 us  [on_device(): pl.pallas_call(functools.partial(kernel, cfg), name='router_backward', ou...]
    unnamed x4 -> x0, waiting for transfers between devices: 55.1 us -> none
    gather x7 -> x0, local copies, waits for them, and re-layouts: 27 us -> none  [the longest x2 20.2 us: on_device(): picked = jnp.take(flat_rows, row_index, axis=0)]
    dot_general x5 -> x1, matrix products: 12.6 us -> 2.2 us  [on_device(): lax.dot_general(lg, router_weight, (((0,), (1,)), ((), ())), preferred_el...]
    reshape x1, local copies, waits for them, and re-layouts: 9.32 us -> 1.34 us  [on_device(): router_bias.reshape(experts, 1)]
    all_to_all x1 -> x0, starting transfers between devices: 7.45 us -> none  [on_device(): lax.all_to_all(expert_rows, 'ep', split_axis=2, concat_axis=1, tiled=True)]
    unnamed x17 -> x6, local copies, waits for them, and re-layouts: 11.3 us -> 7.47 us
  transfers between devices with their start and end apart: 3 -> 0, of which waited for: 2 -> 0; matrix products, arithmetic and copies ran while one was open for 3% -> 0% of each run, Pallas kernels for 0% -> 0%
where the time goes in v1:
time: 119 us
  Pallas kernels  103 us (87%)
  local copies, waits for them, and re-layouts  10.1 us (8%)
  between operations  3.05 us (3%)
  matrix products  2.2 us (2%)
    pallas_call x1, Pallas kernels, on_device(): pl.pallas_call(functools.partial(kernel, cfg), name='router_backward', ou...  103 us
    unnamed x6, local copies, waits for them, and re-layouts  7.47 us

profile of v1, /device:TPU:0, one launch (start us, length us, event | category | flops | bytes accessed | tf_op | source)
XLA Modules:
  0.0 118.5 jit_solution(3167594416336350698)
XLA Ops:
  1.3 1.3 %pad.4.refs_0_ = s32[8,192]{1,0:T(8,128)} pad(s32[4,192]{1,0:T(4,128)} %bitcast.9, s32[]{:T(128)} %constant.0.clone.1), padding=0_4x0_0 | pad | bytes 9220 | tf_op jit(solution)/shard_map/jit(_pad)/pad | solution.py:399
  2.6 1.3 %copy.11.refs_5_ = f32[32,1]{1,0:T(8,128)} copy(f32[32,1]{0,1:T(1,128)} %bitcast.10) | data formatting | bytes 256 | tf_op jit(solution)/shard_map/reshape | solution.py:448
  3.9 6.9 %copy.10.refs_2_ = bf16[1,4,8,36,2880]{4,3,2,1,0:T(8,128)(2,1)} copy(bf16[1,4,8,36,2880]{4,2,3,1,0:T(8,128)(2,1)} %param.10) | data formatting | bytes 13271040 | tf_op args[3]
  10.8 0.0 copy-start
  10.8 103.2 %router_backward.1 = (bf16[32,192]{1,0:T(8,128)(2,1)}, f32[4,720]{1,0:T(4,128)}, f32[1,1]{1,0:T(1,128)}) custom-call(s32[8,192]{1,0:T(8,128)} %pad.4.refs_0_, bf16[192,2880]{1,0:T(8,128)(2,1)} %refs_1_.1, bf16[1,4,8,36,2880]{4,3,2,1,0:T(8,128)(2,1)} %copy.10.refs_2_, bf16[192,2880]{1,0:T(8,128)(2,1)} %refs_3_.1, bf16[32,2880]{1,0:T(8,128)(2,1)} %bitcast.7, ...), custom_call_target="tpu_custom_call" | custom-call | tf_op jit(solution)/shard_map/router_backward/pallas_call | solution.py:434
  114.0 0.0 copy-start.1
  114.0 0.0 copy-done
  114.0 2.2 %convolution_convert_fusion = bf16[192,2880]{1,0:T(8,128)(2,1)} fusion(bf16[32,192]{1,0:T(8,128)(2,1)} %get-tuple-element.6, bf16[2880,32]{0,1:T(8,128)(2,1)S(1)} %copy-done), kind=kOutput, calls=%fused_computation | convolution fusion | flops 35942400 | bytes 1302528 | tf_op jit(solution)/shard_map/dot_general | solution.py:449
  116.2 0.0 copy-done.1
  116.2 0.6 copy.15
Async XLA Ops:
  10.8 103.2 %copy-start = (bf16[2880,32]{0,1:T(8,128)(2,1)S(1)}, bf16[2880,32]{0,1:T(8,128)(2,1)}, u32[]{:S(2)}) copy-start(bf16[2880,32]{0,1:T(8,128)(2,1)} %param.11) | copy-start | bytes 552964
  114.0 2.2 %copy-start.1 = (f32[4,720]{1,0:T(4,128)S(1)}, f32[4,720]{1,0:T(4,128)}, u32[]{:S(2)}) copy-start(f32[4,720]{1,0:T(4,128)} %get-tuple-element.7) | copy-start | bytes 34564

commit v2 on v1

--- a/solution.py
+++ b/solution.py
@@ -36,10 +36,11 @@
     xb = refs[:chunks]
     lsend = refs[chunks:2 * chunks]
     lrecv = refs[2 * chunks:3 * chunks]
-    (rows_v, idx_all, pin, pout, tgt_x, tgt_p, acc_x, acc_p, rst, rbuf, tks, tkr, logit_v, prob_v,
+    rows_v = refs[3 * chunks:4 * chunks]
+    (rows_raw, piled, idx_all, pin, pout, tgt_x, tgt_p, acc_x, acc_p, rst, rbuf, tks, tkr, logit_v, prob_v,
      named_v, st_dp, st_ep, lgd, ws, wr,
      s_rows, s_own, s_idx, r_idx, s_right, s_left, r_x, s_leaf, r_leaf, s_rep, r_rep,
-     s_tk, r_tk, s_sd, r_sd, s_se, r_se, s_lg, r_lg, s_w, r_w) = refs[3 * chunks:]
+     s_tk, r_tk, s_sd, r_sd, s_se, r_se, s_lg, r_lg, s_w, r_w) = refs[4 * chunks:]
     me = lax.axis_index("ep")
     md = lax.axis_index("dp")
     pos = me // 2
@@ -66,7 +67,7 @@
     ]
     for copy in own:
         copy.start()
-    rows_copy = pltpu.make_async_copy(rows_in.at[0], rows_v, s_rows)
+    rows_copy = pltpu.make_async_copy(rows_in, rows_raw, s_rows)
     rows_copy.start()
 
     barrier = pltpu.get_barrier_semaphore()
@@ -126,7 +127,13 @@
     named = jnp.zeros((experts, tok_dev), F32)
     for k in range(chosen):
         named = named + jnp.where(idx[k:k + 1, :] == expert_row, 1.0, 0.0)
-    logits = dot_nt(wt_in[...], tok_in[...]) + bias_in[...]
+    eye_r = lax.broadcasted_iota(jnp.int32, (experts, experts), 0)
+    eye_c = lax.broadcasted_iota(jnp.int32, (experts, experts), 1)
+
+    def upright(line_of):
+        return jnp.sum(jnp.where(eye_r == eye_c, line_of, 0.0), axis=1, keepdims=True)
+
+    logits = dot_nt(wt_in[...], tok_in[...]) + upright(bias_in[...])
     top = jnp.max(logits, axis=0, keepdims=True)
     power = jnp.exp(logits - top)
     prob = power / jnp.sum(power, axis=0, keepdims=True)
@@ -197,14 +204,38 @@
     lax.fori_loop(0, line, plans, 0)
     rows_copy.wait()
 
-    def gathered(j, c, block, target, count):
-        slot = lax.broadcasted_iota(jnp.int32, (cap, count), 0).astype(F32)
+    deep = piled.shape[1] // ep
+    slot_r = lax.broadcasted_iota(jnp.int32, (deep, cap * ep), 0)
+    lies = lax.broadcasted_iota(jnp.int32, (deep, cap * ep), 1)
+    order = jnp.concatenate(
+        [jnp.where(jnp.logical_and(lies == slot_r * ep + j, slot_r < cap), 1.0, 0.0) for j in range(ep)], axis=0
+    ).astype(BF16)
+    spare = rows_v[0].shape[1] - exp_dev * cap
+
+    def sort_rows(c):
+        w = widths[c]
+        for e in range(exp_dev):
+            piled[e, :, 0:w] = dot_nn(order, rows_raw[e, :, starts[c]:starts[c] + w])
+
+        def put(j, carry):
+            at = pl.ds(pl.multiple_of(j * deep, 8), deep)
+            pieces = [piled[e, at, 0:w][0:cap, :] for e in range(exp_dev)]
+            if spare:
+                pieces.append(jnp.zeros((spare, w), F32))
+            rows_v[c][j] = jnp.concatenate(pieces, axis=0).astype(BF16)
+            return carry
+
+        lax.fori_loop(0, ep, put, 0)
+
+    def gathered(table, block, target, count):
+        height = table.shape[0]
+        slot = lax.broadcasted_iota(jnp.int32, (height, count), 0).astype(F32)
         row = lax.broadcasted_iota(jnp.int32, (8, count), 0)
+        dots = dot_nt(table, block)
         out = jnp.zeros((8, count), F32)
         for e in range(exp_dev):
-            table = rows_v[e, j, :, starts[c]:starts[c] + widths[c]]
-            dots = dot_nt(table, block)
-            one = jnp.sum(jnp.where(slot == target[e:e + 1, :], dots, 0.0), axis=0, keepdims=True)
+            want = jnp.where(target[e:e + 1, :] >= 0.0, target[e:e + 1, :] + e * cap, -1.0)
+            one = jnp.sum(jnp.where(slot == want, dots, 0.0), axis=0, keepdims=True)
             out = jnp.where(row == e, one, out)
         return out
 
@@ -213,11 +244,11 @@
         leaf(q, c).start()
 
     def use_block(q, c):
-        acc_x[q] += gathered(q * 2 + side, c, xb[c][q], tgt_x[q], tok_dev)
+        acc_x[q] += gathered(rows_v[c][q * 2 + side], xb[c][q], tgt_x[q], tok_dev)
 
     def use_leaf(q, c):
         leaf(q, c).wait_recv()
-        acc_p[q] += gathered(q * 2 + 1 - side, c, lrecv[c][q], tgt_p[q], packed)
+        acc_p[q] += gathered(rows_v[c][q * 2 + 1 - side], lrecv[c][q], tgt_p[q], packed)
 
     def answer(j, value):
         rst[j] = value
@@ -251,6 +282,7 @@
     for n, (s, c) in enumerate(steps):
         if s == 0:
             give_leaf(pos, c)
+            sort_rows(c)
             use_block(pos, c)
             if c == chunks - 1:
                 rbuf[me] = acc_x[pos]
@@ -307,9 +339,7 @@
     mean = stats[1:2, :] / token_total
     loss_out[...] = experts * jnp.sum(share * mean, axis=1, keepdims=True)
     push_row = scale_in[0] * experts * share
-    eye_r = lax.broadcasted_iota(jnp.int32, (experts, experts), 0)
-    eye_c = lax.broadcasted_iota(jnp.int32, (experts, experts), 1)
-    push = jnp.sum(jnp.where(eye_r == eye_c, push_row, 0.0), axis=1, keepdims=True)
+    push = upright(push_row)
     prob = prob_v[...]
     spread = prob * (push - jnp.sum(prob * push, axis=0, keepdims=True))
     named = named_v[...]
@@ -396,7 +426,7 @@
     chunks = len(widths)
     cfg = (ep, dp, tok_dev, chosen, experts, exp_dev, cap, packed, widths, tok_dev * ep * dp)
     part = width // dp
-    idx_t = jnp.pad(indices.T, ((0, 8 - chosen), (0, 0)), constant_values=-1)
+    rows_t = jnp.transpose(expert_rows[0], (0, 2, 1, 3)).reshape(exp_dev, cap * ep, width)
     vmem = pl.BlockSpec(memory_space=pltpu.VMEM)
     hbm = pl.BlockSpec(memory_space=pl.ANY)
     smem = pl.BlockSpec(memory_space=pltpu.SMEM)
@@ -404,9 +434,11 @@
     scratch = [pltpu.VMEM((line, tok_dev, w), BF16) for w in widths]
     scratch += [pltpu.VMEM((line, packed, w), BF16) for w in widths]
     scratch += [pltpu.VMEM((line, packed, w), BF16) for w in widths]
+    scratch += [pltpu.VMEM((ep, -(-exp_dev * cap // 16) * 16, w), BF16) for w in widths]
     scratch += [
-        pltpu.VMEM(expert_rows.shape[1:], BF16),
-        pltpu.VMEM((ep, 8, tok_dev), jnp.int32),
+        pltpu.VMEM((exp_dev, cap * ep, width), BF16),
+        pltpu.VMEM((exp_dev, ep * (-(-cap // 8) * 8), widths[0]), F32),
+        pltpu.VMEM((ep, chosen, tok_dev), jnp.int32),
         pltpu.VMEM((line, packed, tok_dev), BF16),
         pltpu.VMEM((line, packed, tok_dev), BF16),
         pltpu.VMEM((line, 8, tok_dev), F32),
@@ -445,7 +477,7 @@
         compiler_params=pltpu.CompilerParams(
             collective_id=0, has_side_effects=True, vmem_limit_bytes=56 * 1024 * 1024
         ),
-    )(idx_t, out_grad, expert_rows, tokens, router_weight.T, router_bias.reshape(experts, 1), balance_scale)
+    )(indices.T, out_grad, rows_t, tokens, router_weight.T, router_bias.reshape(1, experts), balance_scale)
     token_grad = lax.dot_general(
         lg, router_weight, (((0,), (1,)), ((), ())), preferred_element_type=F32
     ).astype(BF16)

time: 119 us -> 109 us (0.916)
  local copies, waits for them, and re-layouts: 10.1 us -> 0.61 us
    unnamed x6 -> x5, local copies, waits for them, and re-layouts: 7.47 us -> 0.61 us
    reshape x1 -> x0, local copies, waits for them, and re-layouts: 1.34 us -> none  [on_device(): router_bias.reshape(experts, 1)]
    pad x1 -> x0, local copies, waits for them, and re-layouts: 1.29 us -> none  [on_device(): idx_t = jnp.pad(indices.T, ((0, 8 - chosen), (0, 0)), constant_values=-1)]
where the time goes in v2:
time: 109 us; the launch traced here: 108 us
  Pallas kernels  103 us (94%)
  between operations  3.06 us (3%)
  matrix products  2.2 us (2%)
    pallas_call x1, Pallas kernels, on_device(): pl.pallas_call(functools.partial(kernel, cfg), name='router_backward', ou...  103 us
    dot_general x1, matrix products, on_device(): lax.dot_general(lg, router_weight, (((0,), (1,)), ((), ())), preferred_el...  2.2 us

profile of v2, /device:TPU:0, one launch (start us, length us, event | category | flops | bytes accessed | tf_op | source)
XLA Modules:
  0.0 108.4 jit_solution(10347459909593397863)
XLA Ops:
  1.3 0.0 copy-start
  1.3 102.6 %router_backward.1 = (bf16[32,192]{1,0:T(8,128)(2,1)}, f32[4,720]{1,0:T(4,128)}, f32[1,1]{1,0:T(1,128)}) custom-call(s32[4,192]{1,0:T(4,128)} %bitcast.15, bf16[192,2880]{1,0:T(8,128)(2,1)} %refs_1_.1, bf16[4,288,2880]{2,1,0:T(8,128)(2,1)} %bitcast.12, bf16[192,2880]{1,0:T(8,128)(2,1)} %refs_3_.1, bf16[32,2880]{1,0:T(8,128)(2,1)} %bitcast.13, ...), custom_call_target="tpu_custom_call" | custom-call | tf_op jit(solution)/shard_map/router_backward/pallas_call | solution.py:466
  103.9 0.0 copy-start.1
  103.9 0.0 copy-done
  103.9 2.2 %convolution_convert_fusion = bf16[192,2880]{1,0:T(8,128)(2,1)} fusion(bf16[32,192]{1,0:T(8,128)(2,1)} %get-tuple-element.6, bf16[2880,32]{0,1:T(8,128)(2,1)S(1)} %copy-done), kind=kOutput, calls=%fused_computation | convolution fusion | flops 35942400 | bytes 1302528 | tf_op jit(solution)/shard_map/dot_general | solution.py:481
  106.1 0.0 copy-done.1
  106.1 0.6 copy.13
Async XLA Ops:
  1.3 102.6 %copy-start = (bf16[2880,32]{0,1:T(8,128)(2,1)S(1)}, bf16[2880,32]{0,1:T(8,128)(2,1)}, u32[]{:S(2)}) copy-start(bf16[2880,32]{0,1:T(8,128)(2,1)} %param.11) | copy-start | bytes 552964
  103.9 2.2 %copy-start.1 = (f32[4,720]{1,0:T(4,128)S(1)}, f32[4,720]{1,0:T(4,128)}, u32[]{:S(2)}) copy-start(f32[4,720]{1,0:T(4,128)} %get-tuple-element.7) | copy-start | bytes 34564

commit v3 on v2

--- a/solution.py
+++ b/solution.py
@@ -37,15 +37,22 @@
     lsend = refs[chunks:2 * chunks]
     lrecv = refs[2 * chunks:3 * chunks]
     rows_v = refs[3 * chunks:4 * chunks]
-    (rows_raw, piled, idx_all, pin, pout, tgt_x, tgt_p, acc_x, acc_p, rst, rbuf, tks, tkr, logit_v, prob_v,
+    back = refs[4 * chunks:5 * chunks]
+    (rows_raw, piled, tgt_r, acc_r, s_back, r_back, idx_all, pin, pout, tgt_x, tgt_p, acc_x, acc_p, rst, rbuf, tks, tkr, logit_v, prob_v,
      named_v, st_dp, st_ep, lgd, ws, wr,
      s_rows, s_own, s_idx, r_idx, s_right, s_left, r_x, s_leaf, r_leaf, s_rep, r_rep,
-     s_tk, r_tk, s_sd, r_sd, s_se, r_se, s_lg, r_lg, s_w, r_w) = refs[4 * chunks:]
+     s_tk, r_tk, s_sd, r_sd, s_se, r_se, s_lg, r_lg, s_w, r_w) = refs[5 * chunks:]
     me = lax.axis_index("ep")
     md = lax.axis_index("dp")
     pos = me // 2
     side = lax.rem(me, 2)
     mate = pos * 2 + 1 - side
+    swapped = range(chunks - 1) if line >= 4 else range(0)
+    last = line - 1
+    at_end = jnp.logical_or(pos == 0, pos == last)
+    near_end = jnp.logical_or(pos == 1, pos == last - 1)
+    end = jnp.where(pos * 2 < line, 0, last)
+    near = jnp.where(pos * 2 < line, 1, last - 1)
 
     def ep_id(other):
         return (other, md)
@@ -103,6 +110,17 @@
     def leaf(q, c):
         return remote(lsend[c].at[q], lrecv[c].at[q], s_leaf.at[q, c], r_leaf.at[q, c], ep_id(mate))
 
+    def send_back(b, c):
+        return remote(rows_v[c].at[near * 2 + b], back[c].at[side], s_back.at[b, c], r_back.at[side, c], ep_id(near * 2 + b))
+
+    def from_left(s, c):
+        ok = pos - s >= 0
+        return jnp.logical_and(ok, pos < last) if s == 1 and c in swapped else ok
+
+    def from_right(s, c):
+        ok = pos + s < line
+        return jnp.logical_and(ok, pos > 0) if s == 1 and c in swapped else ok
+
     def reply(j):
         return remote(rst.at[j], rbuf.at[me], s_rep.at[j], r_rep.at[me], ep_id(j))
 
@@ -110,11 +128,11 @@
     for c in range(chunks):
         own[c].wait()
 
-        @pl.when(pos < line - 1)
+        @pl.when(pos < last - (c in swapped))
         def _():
             to_right(pos, c).start()
 
-        @pl.when(pos > 0)
+        @pl.when(pos > 0 + (c in swapped))
         def _():
             to_left(pos, c).start()
 
@@ -202,6 +220,9 @@
         return carry
 
     lax.fori_loop(0, line, plans, 0)
+    for b in range(2):
+        tgt_r[b], _ = plan(idx, end * 2 + b)
+        acc_r[b] = jnp.zeros((8, tok_dev), F32)
     rows_copy.wait()
 
     deep = piled.shape[1] // ep
@@ -269,11 +290,11 @@
             go(pos)
             return
 
-        @pl.when(pos - s >= 0)
+        @pl.when(from_left(s, c))
         def _():
             go(pos - s)
 
-        @pl.when(pos + s < line)
+        @pl.when(from_right(s, c))
         def _():
             go(pos + s)
 
@@ -283,11 +304,16 @@
         if s == 0:
             give_leaf(pos, c)
             sort_rows(c)
+            if c in swapped:
+                @pl.when(at_end)
+                def _():
+                    for b in range(2):
+                        send_back(b, c).start()
             use_block(pos, c)
             if c == chunks - 1:
                 rbuf[me] = acc_x[pos]
         else:
-            @pl.when(pos - s >= 0)
+            @pl.when(from_left(s, c))
             def _():
                 q = pos - s
                 to_right(q, c).wait_recv()
@@ -296,7 +322,7 @@
                 def _():
                     to_right(q, c).start()
 
-            @pl.when(pos + s < line)
+            @pl.when(from_right(s, c))
             def _():
                 q = pos + s
                 to_left(q, c).wait_recv()
@@ -305,12 +331,12 @@
                 def _():
                     to_left(q, c).start()
 
-            for q, ok in ((pos - s, pos - s >= 0), (pos + s, pos + s < line)):
+            for q, ok in ((pos - s, from_left(s, c)), (pos + s, from_right(s, c))):
                 @pl.when(ok)
                 def _(q=q):
                     give_leaf(q, c)
 
-            for q, ok in ((pos - s, pos - s >= 0), (pos + s, pos + s < line)):
+            for q, ok in ((pos - s, from_left(s, c)), (pos + s, from_right(s, c))):
                 @pl.when(ok)
                 def _(q=q):
                     use_block(q, c)
@@ -318,6 +344,12 @@
                         done_block(q)
         if n >= lag:
             leaf_step(*steps[n - lag])
+        if s == last and c in swapped:
+            @pl.when(near_end)
+            def _():
+                for b in range(2):
+                    remote(back[c].at[b], back[c].at[b], s_back.at[b, c], r_back.at[b, c], ep_id(end * 2 + b)).wait_recv()
+                    acc_r[b] += gathered(back[c][b], xb[c][pos], tgt_r[b], tok_dev)
         if n == 1:
             for s_ in range(1, dp):
                 sd_arrival(s_).wait_recv()
@@ -353,6 +385,11 @@
         remote(rst.at[src], rbuf.at[src], s_rep.at[src], r_rep.at[src], ep_id(src)).wait_recv()
 
     loop_ep(rep_arrival)
+    if len(swapped):
+        @pl.when(near_end)
+        def _():
+            for b in range(2):
+                rbuf[end * 2 + b] += acc_r[b]
     dots = jnp.concatenate([rbuf[j, 0:exp_dev, :] for j in range(ep)], axis=0)
     sel = mix * (dots - jnp.sum(mix * dots, axis=0, keepdims=True))
     grad = (spread + sel).astype(BF16)
@@ -399,17 +436,33 @@
 
     def drain(q, carry):
         for c in range(chunks):
-            leaf(q, c).wait_send()
-
-            @pl.when(jnp.logical_and(q <= pos, pos < line - 1))
+            right = jnp.logical_and(q <= pos, pos < last)
+            left = jnp.logical_and(q >= pos, pos > 0)
+            used = q >= 0
+            if c in swapped:
+                right = jnp.logical_and(right, jnp.logical_or(q < pos, pos < last - 1))
+                left = jnp.logical_and(left, jnp.logical_or(q > pos, pos > 1))
+                used = jnp.logical_not(jnp.logical_and(at_end, q == near))
+
+            @pl.when(used)
+            def _():
+                leaf(q, c).wait_send()
+
+            @pl.when(right)
             def _():
                 to_right(q, c).wait_send()
 
-            @pl.when(jnp.logical_and(q >= pos, pos > 0))
+            @pl.when(left)
             def _():
                 to_left(q, c).wait_send()
         return carry
 
+    if len(swapped):
+        @pl.when(at_end)
+        def _():
+            for c in swapped:
+                for b in range(2):
+                    send_back(b, c).wait_send()
     lax.fori_loop(0, line, drain, 0)
 
 
@@ -435,9 +488,13 @@
     scratch += [pltpu.VMEM((line, packed, w), BF16) for w in widths]
     scratch += [pltpu.VMEM((line, packed, w), BF16) for w in widths]
     scratch += [pltpu.VMEM((ep, -(-exp_dev * cap // 16) * 16, w), BF16) for w in widths]
+    scratch += [pltpu.VMEM((2, -(-exp_dev * cap // 16) * 16, w), BF16) for w in widths]
     scratch += [
         pltpu.VMEM((exp_dev, cap * ep, width), BF16),
         pltpu.VMEM((exp_dev, ep * (-(-cap // 8) * 8), widths[0]), F32),
+        pltpu.VMEM((2, 8, tok_dev), F32),
+        pltpu.VMEM((2, 8, tok_dev), F32),
+        dma((2, chunks)), dma((2, chunks)),
         pltpu.VMEM((ep, chosen, tok_dev), jnp.int32),
         pltpu.VMEM((line, packed, tok_dev), BF16),
         pltpu.VMEM((line, packed, tok_dev), BF16),

time: 109 us -> 109 us (level)
  no operation moved by 1% of the time
where the time goes in v3:
time: 109 us
  Pallas kernels  103 us (94%)
  between operations  3.06 us (3%)
  matrix products  2.2 us (2%)
    pallas_call x1, Pallas kernels, on_device(): pl.pallas_call(functools.partial(kernel, cfg), name='router_backward', ou...  103 us
    dot_general x1, matrix products, on_device(): lax.dot_general(lg, router_weight, (((0,), (1,)), ((), ())), preferred_el...  2.2 us

profile of v3, /device:TPU:0, one launch (start us, length us, event | category | flops | bytes accessed | tf_op | source)
XLA Modules:
  0.0 108.5 jit_solution(15509936882165305189)
XLA Ops:
  1.3 0.0 copy-start
  1.3 102.6 %router_backward.1 = (bf16[32,192]{1,0:T(8,128)(2,1)}, f32[4,720]{1,0:T(4,128)}, f32[1,1]{1,0:T(1,128)}) custom-call(s32[4,192]{1,0:T(4,128)} %bitcast.15, bf16[192,2880]{1,0:T(8,128)(2,1)} %refs_1_.1, bf16[4,288,2880]{2,1,0:T(8,128)(2,1)} %bitcast.12, bf16[192,2880]{1,0:T(8,128)(2,1)} %refs_3_.1, bf16[32,2880]{1,0:T(8,128)(2,1)} %bitcast.13, ...), custom_call_target="tpu_custom_call" | custom-call | tf_op jit(solution)/shard_map/router_backward/pallas_call | solution.py:523
  103.9 0.0 copy-start.1
  104.0 0.0 copy-done
  104.0 2.2 %convolution_convert_fusion = bf16[192,2880]{1,0:T(8,128)(2,1)} fusion(bf16[32,192]{1,0:T(8,128)(2,1)} %get-tuple-element.6, bf16[2880,32]{0,1:T(8,128)(2,1)S(1)} %copy-done), kind=kOutput, calls=%fused_computation | convolution fusion | flops 35942400 | bytes 1302528 | tf_op jit(solution)/shard_map/dot_general | solution.py:538
  106.2 0.0 copy-done.1
  106.2 0.6 copy.13
Async XLA Ops:
  1.3 102.7 %copy-start = (bf16[2880,32]{0,1:T(8,128)(2,1)S(1)}, bf16[2880,32]{0,1:T(8,128)(2,1)}, u32[]{:S(2)}) copy-start(bf16[2880,32]{0,1:T(8,128)(2,1)} %param.11) | copy-start | bytes 552964
  103.9 2.2 %copy-start.1 = (f32[4,720]{1,0:T(4,128)S(1)}, f32[4,720]{1,0:T(4,128)}, u32[]{:S(2)}) copy-start(f32[4,720]{1,0:T(4,128)} %get-tuple-element.7) | copy-start | bytes 34564

commit v4 on v3

--- a/solution.py
+++ b/solution.py
@@ -47,7 +47,7 @@
     pos = me // 2
     side = lax.rem(me, 2)
     mate = pos * 2 + 1 - side
-    swapped = range(chunks - 1) if line >= 4 else range(0)
+    swapped = range(min(1, chunks - 1)) if line >= 4 else range(0)
     last = line - 1
     at_end = jnp.logical_or(pos == 0, pos == last)
     near_end = jnp.logical_or(pos == 1, pos == last - 1)

time: 109 us -> 102 us (0.936)
  Pallas kernels: 103 us -> 95.9 us
    pallas_call x1, Pallas kernels: 103 us -> 95.9 us  [on_device(): pl.pallas_call(functools.partial(kernel, cfg), name='router_backward', ou...]
where the time goes in v4:
time: 102 us
  Pallas kernels  95.9 us (94%)
  between operations  3.06 us (3%)
  matrix products  2.2 us (2%)
    pallas_call x1, Pallas kernels, on_device(): pl.pallas_call(functools.partial(kernel, cfg), name='router_backward', ou...  95.9 us
    dot_general x1, matrix products, on_device(): lax.dot_general(lg, router_weight, (((0,), (1,)), ((), ())), preferred_el...  2.2 us

profile of v4, /device:TPU:0, one launch (start us, length us, event | category | flops | bytes accessed | tf_op | source)
XLA Modules:
  0.0 101.8 jit_solution(1201164732426557908)
XLA Ops:
  1.3 0.0 copy-start
  1.3 95.9 %router_backward.1 = (bf16[32,192]{1,0:T(8,128)(2,1)}, f32[4,720]{1,0:T(4,128)}, f32[1,1]{1,0:T(1,128)}) custom-call(s32[4,192]{1,0:T(4,128)} %bitcast.15, bf16[192,2880]{1,0:T(8,128)(2,1)} %refs_1_.1, bf16[4,288,2880]{2,1,0:T(8,128)(2,1)} %bitcast.12, bf16[192,2880]{1,0:T(8,128)(2,1)} %refs_3_.1, bf16[32,2880]{1,0:T(8,128)(2,1)} %bitcast.13, ...), custom_call_target="tpu_custom_call" | custom-call | tf_op jit(solution)/shard_map/router_backward/pallas_call | solution.py:523
  97.2 0.0 copy-start.1
  97.2 0.0 copy-done
  97.2 2.2 %convolution_convert_fusion = bf16[192,2880]{1,0:T(8,128)(2,1)} fusion(bf16[32,192]{1,0:T(8,128)(2,1)} %get-tuple-element.6, bf16[2880,32]{0,1:T(8,128)(2,1)S(1)} %copy-done), kind=kOutput, calls=%fused_computation | convolution fusion | flops 35942400 | bytes 1302528 | tf_op jit(solution)/shard_map/dot_general | solution.py:538
  99.4 0.0 copy-done.1
  99.4 0.6 copy.13
Async XLA Ops:
  1.3 95.9 %copy-start = (bf16[2880,32]{0,1:T(8,128)(2,1)S(1)}, bf16[2880,32]{0,1:T(8,128)(2,1)}, u32[]{:S(2)}) copy-start(bf16[2880,32]{0,1:T(8,128)(2,1)} %param.11) | copy-start | bytes 552964
  97.2 2.2 %copy-start.1 = (f32[4,720]{1,0:T(4,128)S(1)}, f32[4,720]{1,0:T(4,128)}, u32[]{:S(2)}) copy-start(f32[4,720]{1,0:T(4,128)} %get-tuple-element.7) | copy-start | bytes 34564
